TPU v7x, 32 devices: a whole 2x2x4 slice. The times are simulated.
32 devices in a mesh: dist: 4 (over y, core), pix: 8 (over z, x).
Axes of the slice: x: 2, y: 2, z: 4, core: 2. Of those that a mesh axis runs over, the one named last changes fastest.
Arguments:
- contrast: float32 [4, 2, 2048, 2048], P('dist', None, 'pix'), may hold values from -6 to 6
- defocus: float32 [4], P('dist'), may hold values from 40 to 400
- blurring: float32 [4], P('dist'), may hold values from 0.5 to 4
Outputs:
- phase: float32 [2, 2048, 2048], P(None, 'pix')
All inputs are finite; a program needn't handle non-finite values.
Results may differ from a plain program's by a relative error of at most 0.0003.
Values sent between devices are 32-bit elements; how exact they have to be, the bound alone decides.
A program may use at most 64 MiB of HBM per device.

v0:
```python
import math
import jax
import jax.numpy as jnp
from jax import lax
from jax.sharding import PartitionSpec as P

ABSORB_RATIO = 0.1
REGULARIZER = 0.05


def unit_phase(first_len, second_len, period):
    left_index = jnp.arange(first_len, dtype=jnp.int32)[:, None]
    right_index = jnp.arange(second_len, dtype=jnp.int32)[None, :]
    turn_count = left_index * right_index % period
    angles = 2.0 * math.pi / period * turn_count.astype(jnp.float32)
    return (jnp.cos(angles), -jnp.sin(angles))


def conjugate_flip(tables):
    return (tables[0], -tables[1])


def complex_product(pattern, real_part, imag_part, tables):
    cosine, sine_part = tables
    out_real = jnp.einsum(pattern, real_part, cosine, precision=lax.Precision.HIGHEST) - jnp.einsum(
        pattern, imag_part, sine_part, precision=lax.Precision.HIGHEST
    )
    out_imag = jnp.einsum(
        pattern, real_part, sine_part, precision=lax.Precision.HIGHEST
    ) + jnp.einsum(pattern, imag_part, cosine, precision=lax.Precision.HIGHEST)
    return (out_real, out_imag)


def apply_twist(real_part, imag_part, cosine, sine_part):
    return (real_part * cosine - imag_part * sine_part, real_part * sine_part + imag_part * cosine)


def signed_square(freq_index, period):
    shifted = freq_index - period * (2 * freq_index >= period).astype(jnp.int32)
    fraction = shifted.astype(jnp.float32) / period
    return fraction * fraction


def transfer(defocus_value, blur_rate, squared):
    return jnp.exp(-blur_rate * squared) * (
        jnp.sin(defocus_value * squared) + ABSORB_RATIO * jnp.cos(defocus_value * squared)
    )


def body(contrast, defocus, blurring):
    images = contrast[0]
    projections, rows_local, columns = images.shape
    pix_count = lax.axis_size("pix")
    col_block = columns // pix_count
    rows_total = rows_local * pix_count
    outer_table = unit_phase(col_block, col_block, col_block)
    pixel_lookup_table = unit_phase(pix_count, pix_count, pix_count)
    row_table = unit_phase(rows_local, rows_local, rows_local)
    col_twist = unit_phase(col_block, pix_count, columns)
    row_twist = unit_phase(rows_local, pix_count, rows_total)
    even_images = images[0::2]
    odd_images = images[1::2]
    shaped_real = even_images.reshape(projections // 2, rows_local, col_block, pix_count)
    shaped_imag = odd_images.reshape(projections // 2, rows_local, col_block, pix_count)
    section_real, section_imag = complex_product(
        "prbn,bc->pcrn", shaped_real, shaped_imag, outer_table
    )
    section_real, section_imag = apply_twist(
        section_real, section_imag, col_twist[0][:, None, :], col_twist[1][:, None, :]
    )
    spec_real, spec_imag = complex_product(
        "pcrn,nq->pcrq", section_real, section_imag, pixel_lookup_table
    )
    col_freq = col_block * lax.axis_index("pix") + jnp.arange(col_block, dtype=jnp.int32)
    row_freq = (
        pix_count * jnp.arange(rows_local, dtype=jnp.int32)[:, None]
        + jnp.arange(pix_count, dtype=jnp.int32)[None, :]
    )
    squared = (
        signed_square(row_freq, rows_total)[None, :, :]
        + signed_square(col_freq, columns)[:, None, None]
    )
    own_gain = transfer(defocus[0], blurring[0], squared)
    received_real = lax.all_to_all(spec_real, "pix", split_axis=3, concat_axis=3, tiled=True)
    received_imaginary = lax.all_to_all(spec_imag, "pix", split_axis=3, concat_axis=3, tiled=True)
    middle_real, middle_imaginary = complex_product(
        "uhqb,bn->uhqn", received_real, received_imaginary, pixel_lookup_table
    )
    middle_real, middle_imaginary = apply_twist(
        middle_real, middle_imaginary, row_twist[0], row_twist[1]
    )
    out_real, out_imag = complex_product("pcrk,rj->pcjk", middle_real, middle_imaginary, row_table)
    summands = (own_gain * out_real, own_gain * out_imag, (own_gain * own_gain)[None])
    totals = lax.psum((summands[0], summands[1], summands[2]), "dist")
    den_sum = totals[2][0]
    bottom = 2.0 * (den_sum + REGULARIZER)
    quot_real = totals[0] / bottom
    quot_imag = totals[1] / bottom
    backward_real, backward_imaginary = complex_product(
        "pcjk,rj->pcrk", quot_real, quot_imag, conjugate_flip(row_table)
    )
    backward_real, backward_imaginary = apply_twist(
        backward_real, backward_imaginary, row_twist[0], -row_twist[1]
    )
    backward_real, backward_imaginary = complex_product(
        "uotv,zv->uotz", backward_real, backward_imaginary, conjugate_flip(pixel_lookup_table)
    )
    backward_real = backward_real / rows_total
    backward_imaginary = backward_imaginary / rows_total
    twist_cos = col_twist[0]
    twist_sin = col_twist[1]
    received_real = lax.all_to_all(backward_real, "pix", split_axis=3, concat_axis=3, tiled=True)
    received_imaginary = lax.all_to_all(
        backward_imaginary, "pix", split_axis=3, concat_axis=3, tiled=True
    )
    middle_real, middle_imaginary = complex_product(
        "pcrq,nq->pcrn", received_real, received_imaginary, conjugate_flip(pixel_lookup_table)
    )
    cols_real, cols_imag = apply_twist(
        middle_real, middle_imaginary, twist_cos[:, None, :], -twist_sin[:, None, :]
    )
    phase_blocks = jnp.einsum(
        "pcrn,cb->prbn", cols_real, outer_table[0], precision=lax.Precision.HIGHEST
    ) + jnp.einsum("pcrn,cb->prbn", cols_imag, outer_table[1], precision=lax.Precision.HIGHEST)
    odd_blocks = jnp.einsum(
        "pcrn,cb->prbn", cols_imag, outer_table[0], precision=lax.Precision.HIGHEST
    ) - jnp.einsum("pcrn,cb->prbn", cols_real, outer_table[1], precision=lax.Precision.HIGHEST)
    paired_blocks = jnp.stack([phase_blocks, odd_blocks], axis=1)
    return (paired_blocks / columns).reshape(projections, rows_local, columns)


def solution(mesh):
    return jax.shard_map(
        body,
        mesh=mesh,
        in_specs=(P("dist", None, "pix", None), P("dist"), P("dist")),
        out_specs=P(None, "pix", None),
        check_vma=False,
    )
```

profile of v0, /device:TPU:0, one launch (start us, length us, event | category | flops | bytes accessed | tf_op | source)
XLA Modules:
  0.0 490.3 jit_solution(7486254267559087429)
XLA Ops:
  6.6 3.9 fusion.322
  14.3 4.2 fusion.102
  18.5 4.2 fusion.90
  27.8 5.4 %convolution_subtract_fusion = f32[256,256,8]{1,0,2:T(8,128)S(1)} fusion(f32[256,256,8]{1,0,2:T(8,128)} %fusion.102, f32[256,256,8]{1,0,2:T(8,128)S(1)} %copy.80), kind=kOutput, calls=%fused_computation.91 | convolution fusion | flops 1612120064 | bytes 6291456 | tf_op jit(solution)/shard_map/prbn,bc->pcrn/dot_general | solution.py:25
  33.2 5.2 %multiply_subtract_fusion.2 = (f32[256,256,8]{1,0,2:T(8,128)S(1)}, f32[256,256,8]{1,0,2:T(8,128)S(1)}) fusion(f32[256,256,8]{1,0,2:T(8,128)S(1)} %convolution_subtract_fusion, f32[256,8]{0,1:T(8,128)S(1)} %get-tuple-element.19, f32[256,8]{0,1:T(8,128)S(1)} %get-tuple-element.18, f32[256,256,8]{1,0,2:T(8,128)S(1)} %copy-done.4, f32[256,256,8]{1,0,2:T(8,128)} %copy-done), kind=kOutput, calls=%fused_computation.59 | convolution fusion | flops 1615200256 | bytes 10502144 | tf_op jit(solution)/shard_map/prbn,bc->pcrn/dot_general | solution.py:30
  41.6 3.6 add_bitcast_fusion.1
  47.1 7.3 %all-to-all-start.1 = ((f32[1,256,256,8]{2,1,0,3:T(8,128)}), f32[1,256,256,8]{2,1,0,3:T(8,128)}, u32[]{:S(2)}, u32[]{:S(2)}) async-start(f32[1,256,256,8]{2,1,0,3:T(8,128)} %copy.94), calls=%async_computation.1 | async-start | bytes 4194304 | tf_op jit(solution)/shard_map/all_to_all | solution.py:85
  54.4 4.7 fusion.52
  64.3 38.4 %all-to-all-done.1 = f32[1,256,256,8]{2,1,0,3:T(8,128)} async-done(((f32[1,256,256,8]{2,1,0,3:T(8,128)}), f32[1,256,256,8]{2,1,0,3:T(8,128)}, u32[]{:S(2)}, u32[]{:S(2)}) %all-to-all-start.1) | async-done | bytes 2097184 | tf_op jit(solution)/shard_map/all_to_all | solution.py:85
  102.7 3.6 all-to-all-start
  107.8 9.4 %fusion.80 = f32[1,256,256,8]{1,2,3,0:T(8,128)} fusion(f32[]{:T(128)} %bitcast.201, f32[256]{0:T(256)S(1)} %fusion.189, f32[256,8]{0,1:T(8,128)S(1)} %multiply_multiply_fusion, f32[]{:T(128)} %bitcast.2), kind=kLoop, calls=%fused_computation.92 | loop fusion | flops 3670016 | bytes 2106376 | tf_op jit(solution)/shard_map/mul | solution.py:93
  117.2 6.0 %fusion.28 = f32[256,256,8]{1,2,0:T(8,128)} fusion(f32[1,256,256,8]{2,1,0,3:T(8,128)} %all-to-all-done.1), kind=kOutput, calls=%fused_computation.37 | convolution fusion | flops 50332608 | bytes 4194304 | tf_op jit(solution)/shard_map/uhqb,bn->uhqn/dot_general | solution.py:25
  123.2 6.1 %fusion.26 = f32[256,256,8]{1,2,0:T(8,128)} fusion(f32[1,256,256,8]{2,1,0,3:T(8,128)} %all-to-all-done.1), kind=kOutput, calls=%fused_computation.35 | convolution fusion | flops 50332544 | bytes 4194304 | tf_op jit(solution)/shard_map/uhqb,bn->uhqn/dot_general | solution.py:30
  129.2 25.6 %all-to-all-done = f32[1,256,256,8]{2,1,0,3:T(8,128)S(1)} async-done(((f32[1,256,256,8]{2,1,0,3:T(8,128)}), f32[1,256,256,8]{2,1,0,3:T(8,128)S(1)}, u32[]{:S(2)}, u32[]{:S(2)}) %all-to-all-start) | async-done | bytes 2097184 | tf_op jit(solution)/shard_map/all_to_all | solution.py:84
  154.8 5.1 %fusion.68 = f32[256,256,8]{1,2,0:T(8,128)S(1)} fusion(f32[256,256,8]{1,2,0:T(8,128)} %fusion.28, f32[1,256,256,8]{2,1,0,3:T(8,128)S(1)} %all-to-all-done), kind=kOutput, calls=%fused_computation.86 | convolution fusion | flops 50856832 | bytes 6291456 | tf_op jit(solution)/shard_map/uhqb,bn->uhqn/dot_general | solution.py:25
  159.9 3.8 multiply_subtract_fusion.1
  170.3 13.1 %bitcast_multiply_fusion.1 = f32[1,256,256,8]{1,2,3,0:T(8,128)} fusion(f32[256,256,8]{1,0,2:T(8,128)S(1)} %fusion.40, f32[256,256,8]{1,2,0:T(8,128)S(1)} %get-tuple-element.12, f32[]{:T(128)} %bitcast.200, f32[256]{0:T(256)S(1)} %fusion.189, f32[256,8]{0,1:T(8,128)S(1)} %multiply_multiply_fusion, f32[]{:T(128)} %bitcast.2), kind=kOutput, calls=%fused_computation.10 | convolution fusion | flops 1615724544 | bytes 6300680 | tf_op jit(solution)/shard_map/pcrk,rj->pcjk/dot_general | solution.py:25
  183.4 12.9 %bitcast_multiply_fusion = f32[1,256,256,8]{1,2,3,0:T(8,128)} fusion(f32[256,256,8]{1,0,2:T(8,128)S(1)} %fusion.38, f32[256,256,8]{1,2,0:T(8,128)S(1)} %get-tuple-element.12, f32[]{:T(128)} %bitcast.202, f32[256]{0:T(256)S(1)} %fusion.189, f32[256,8]{0,1:T(8,128)S(1)} %multiply_multiply_fusion, f32[]{:T(128)} %bitcast.2), kind=kOutput, calls=%fused_computation.9 | convolution fusion | flops 1615790080 | bytes 6300680 | tf_op jit(solution)/shard_map/pcrk,rj->pcjk/dot_general | solution.py:28
  196.4 118.8 %all-reduce.3.cloned.1.call-done = (f32[1,256,256,8]{1,2,3,0:T(8,128)}, f32[1,256,256,8]{1,2,3,0:T(8,128)}, f32[1,256,256,8]{1,2,3,0:T(8,128)}) async-done(((f32[1,256,256,8]{1,2,3,0:T(8,128)}, f32[1,256,256,8]{1,2,3,0:T(8,128)}, f32[1,256,256,8]{1,2,3,0:T(8,128)}), (f32[1,256,256,8]{1,2,3,0:T(8,128)}, f32[1,256,256,8]{1,2,3,0:T(8,128)}, f32[1,256,256,8]{1,2,3,0:T(8,128)})) %all-reduce.3.cloned.1.call-update) | async-done | bytes 6291472 | tf_op jit(solution)/shard_map/psum | solution.py:94
  315.2 5.4 %fusion.18 = f32[256,256,8]{1,0,2:T(8,128)S(1)} fusion(f32[1,256,256,8]{1,2,3,0:T(8,128)} %get-tuple-element.5, f32[1,256,256,8]{1,2,3,0:T(8,128)} %get-tuple-element.6), kind=kOutput, calls=%fused_computation.27 | convolution fusion | flops 1613103104 | bytes 6291456 | tf_op jit(solution)/shard_map/pcjk,rj->pcrk/dot_general | solution.py:30
  320.7 3.3 fusion.20
  327.2 5.7 %fusion.17 = (f32[256,256,8]{0,1,2:T(8,128)}, f32[256,256,8]{0,1,2:T(8,128)}) fusion(f32[256,256,8]{1,0,2:T(8,128)S(1)} %fusion.74, f32[256,8]{0,1:T(8,128)S(1)} %fusion.160, f32[256,8]{0,1:T(8,128)S(1)} %get-tuple-element.18, f32[256,256,8]{1,0,2:T(8,128)S(1)} %fusion.18, f32[1,256,256,8]{1,2,3,0:T(8,128)S(1)} %copy-done.8, ...), kind=kOutput, calls=%fused_computation.24 | convolution fusion | flops 1616773120 | bytes 12599296 | tf_op jit(solution)/shard_map/pcjk,rj->pcrk/dot_general | solution.py:28
  340.9 3.6 multiply_bitcast_fusion.1
  346.5 5.5 %all-to-all-start.2 = ((f32[1,256,256,8]{2,1,0,3:T(8,128)}), f32[1,256,256,8]{2,1,0,3:T(8,128)}, u32[]{:S(2)}, u32[]{:S(2)}) async-start(f32[1,256,256,8]{2,1,0,3:T(8,128)} %copy.113), calls=%async_computation.2 | async-start | bytes 4194304 | tf_op jit(solution)/shard_map/all_to_all | solution.py:112
  352.0 3.5 fusion.142
  359.6 40.4 %all-to-all-done.2 = f32[1,256,256,8]{2,1,0,3:T(8,128)} async-done(((f32[1,256,256,8]{2,1,0,3:T(8,128)}), f32[1,256,256,8]{2,1,0,3:T(8,128)}, u32[]{:S(2)}, u32[]{:S(2)}) %all-to-all-start.2) | async-done | bytes 2097184 | tf_op jit(solution)/shard_map/all_to_all | solution.py:112
  400.0 3.8 all-to-all-start.3
  403.8 6.1 %fusion.10 = f32[256,256,8]{1,2,0:T(8,128)} fusion(f32[1,256,256,8]{2,1,0,3:T(8,128)} %all-to-all-done.2), kind=kOutput, calls=%fused_computation.15 | convolution fusion | flops 50332544 | bytes 4194304 | tf_op jit(solution)/shard_map/pcrq,nq->pcrn/dot_general | solution.py:28
  409.9 5.9 %fusion.12 = f32[256,256,8]{1,2,0:T(8,128)} fusion(f32[1,256,256,8]{2,1,0,3:T(8,128)} %all-to-all-done.2), kind=kOutput, calls=%fused_computation.17 | convolution fusion | flops 50332544 | bytes 4194304 | tf_op jit(solution)/shard_map/pcrq,nq->pcrn/dot_general | solution.py:25
  415.8 36.3 %all-to-all-done.3 = f32[1,256,256,8]{2,1,0,3:T(8,128)S(1)} async-done(((f32[1,256,256,8]{2,1,0,3:T(8,128)}), f32[1,256,256,8]{2,1,0,3:T(8,128)S(1)}, u32[]{:S(2)}, u32[]{:S(2)}) %all-to-all-start.3) | async-done | bytes 2097184 | tf_op jit(solution)/shard_map/all_to_all | solution.py:113
  455.1 3.3 fusion.8
  477.7 5.3 %copy.125 = f32[2,256,2048]{2,1,0:T(8,128)} copy(f32[2,256,2048]{1,2,0:T(8,128)} %maximum_multiply_fusion) | data formatting | bytes 8388608 | tf_op jit(solution)/shard_map/div | solution.py:129
  (53 shorter events, 65.4 us)
Async XLA Ops:
  27.8 5.4 %copy-start = (f32[256,256,8]{1,0,2:T(8,128)}, f32[256,256,8]{1,0,2:T(8,128)S(1)}, u32[]{:S(2)}) copy-start(f32[256,256,8]{1,0,2:T(8,128)S(1)} %copy.80) | copy-start | bytes 6291460
  27.8 5.4 %copy-start.4 = (f32[256,256,8]{1,0,2:T(8,128)S(1)}, f32[256,256,8]{1,0,2:T(8,128)}, u32[]{:S(2)}) copy-start(f32[256,256,8]{1,0,2:T(8,128)} %fusion.90) | copy-start | bytes 6291460
  38.4 3.2 copy-start.1
  47.1 55.6 %all-to-all-start.1 = ((f32[1,256,256,8]{2,1,0,3:T(8,128)}), f32[1,256,256,8]{2,1,0,3:T(8,128)}, u32[]{:S(2)}, u32[]{:S(2)}) async-start(f32[1,256,256,8]{2,1,0,3:T(8,128)} %copy.94), calls=%async_computation.1 | async-start | bytes 4194304 | tf_op jit(solution)/shard_map/all_to_all | solution.py:85
  102.7 52.1 %all-to-all-start = ((f32[1,256,256,8]{2,1,0,3:T(8,128)}), f32[1,256,256,8]{2,1,0,3:T(8,128)S(1)}, u32[]{:S(2)}, u32[]{:S(2)}) async-start(f32[1,256,256,8]{2,1,0,3:T(8,128)} %copy.87), calls=%async_computation | async-start | bytes 4194304 | tf_op jit(solution)/shard_map/all_to_all | solution.py:84
  106.4 208.8 %all-reduce.3.cloned.1.call-start = ((), (), s32[]{:S(2)}) async-start(), calls=%async_computation.4 | async-start | bytes 12582912 | tf_op jit(solution)/shard_map/psum | solution.py:94
  154.8 5.1 %copy-start.3 = (f32[256,256,8]{1,2,0:T(8,128)S(1)}, f32[256,256,8]{1,2,0:T(8,128)}, u32[]{:S(2)}) copy-start(f32[256,256,8]{1,2,0:T(8,128)} %fusion.26) | copy-start | bytes 6291460
  315.2 5.5 %copy-start.7 = (f32[1,256,256,8]{1,2,3,0:T(8,128)S(1)}, f32[1,256,256,8]{1,2,3,0:T(8,128)}, u32[]{:S(2)}) copy-start(f32[1,256,256,8]{1,2,3,0:T(8,128)} %get-tuple-element.6) | copy-start | bytes 6291460
  315.2 5.5 %copy-start.9 = (f32[1,256,256,8]{1,2,3,0:T(8,128)S(1)}, f32[1,256,256,8]{1,2,3,0:T(8,128)}, u32[]{:S(2)}) copy-start(f32[1,256,256,8]{1,2,3,0:T(8,128)} %get-tuple-element.5) | copy-start | bytes 6291460
  320.7 3.3 copy-start.8
  335.1 3.2 copy-start.2
  346.5 53.5 %all-to-all-start.2 = ((f32[1,256,256,8]{2,1,0,3:T(8,128)}), f32[1,256,256,8]{2,1,0,3:T(8,128)}, u32[]{:S(2)}, u32[]{:S(2)}) async-start(f32[1,256,256,8]{2,1,0,3:T(8,128)} %copy.113), calls=%async_computation.2 | async-start | bytes 4194304 | tf_op jit(solution)/shard_map/all_to_all | solution.py:112
  400.0 52.1 %all-to-all-start.3 = ((f32[1,256,256,8]{2,1,0,3:T(8,128)}), f32[1,256,256,8]{2,1,0,3:T(8,128)S(1)}, u32[]{:S(2)}, u32[]{:S(2)}) async-start(f32[1,256,256,8]{2,1,0,3:T(8,128)} %copy.117), calls=%async_computation.3 | async-start | bytes 4194304 | tf_op jit(solution)/shard_map/all_to_all | solution.py:113
  455.1 3.3 copy-start.5
  455.1 3.3 copy-start.6
Sparse Core Ops, SparseCore 0:
  196.4 118.6 all-reduce.2
where the time goes:
time: 497 us; the launch traced here: 490 us
  waiting for transfers between devices  260 us (52%)
  matrix products  147 us (30%)
  local copies, waits for them, and re-layouts  33.6 us (7%)
  starting transfers between devices  20.2 us (4%)
  between operations  15.5 us (3%)
  other arithmetic  14.5 us (3%)
    psum x1, waiting for transfers between devices, body(): totals = lax.psum((summands[0], summands[1], summands[2]), 'dist')  119 us
    all_to_all x1, waiting for transfers between devices, body(): lax.all_to_all(backward_real, 'pix', split_axis=3, concat_axis=3, tiled=T...  40.4 us
    dot_general x7, matrix products, complex_product(): jnp.einsum(pattern, real_part, sine_part, precision=lax.Precision.HIGHEST)  39.8 us
    all_to_all x1, waiting for transfers between devices, body(): lax.all_to_all(spec_imag, 'pix', split_axis=3, concat_axis=3, tiled=True)  38.4 us
    dot_general x7, matrix products, complex_product(): jnp.einsum(pattern, real_part, cosine, precision=lax.Precision.HIGHEST)  37.9 us
    all_to_all x1, waiting for transfers between devices, body(): lax.all_to_all(backward_imaginary, 'pix', split_axis=3, concat_axis=3, ti...  36.3 us
    dot_general x7, matrix products, complex_product(): jnp.einsum(pattern, imag_part, sine_part, precision=lax.Precision.HIGHEST)  29.5 us
    dot_general x7, matrix products, complex_product(): jnp.einsum(pattern, imag_part, cosine, precision=lax.Precision.HIGHEST)  28.2 us
  transfers between devices with their start and end apart: 5, of which 5 were waited for; matrix products, arithmetic and copies ran while one was open for 10% of the time, Pallas kernels for 0%

commit v1 on v0

--- a/solution.py
+++ b/solution.py
@@ -6,6 +6,18 @@
 
 ABSORB_RATIO = 0.1
 REGULARIZER = 0.05
+
+
+def _note_leaves(arr_in, axis_no, x_local):
+    local_now, back = (arr_in.shape[:axis_no], arr_in.shape[axis_no + 1 :])
+    arr_next = arr_in.reshape(*local_now, x_local, -1, *back)
+    return jnp.moveaxis(arr_next, axis_no, 0)
+
+
+def process_ways(mine_x, k_dim):
+    mine_x = jnp.moveaxis(mine_x, 0, k_dim)
+    odd = mine_x.shape
+    return mine_x.reshape(*odd[:k_dim], odd[k_dim] * odd[k_dim + 1], *odd[k_dim + 2 :])
 
 
 def unit_phase(first_len, second_len, period):
@@ -81,7 +93,20 @@
         + signed_square(col_freq, columns)[:, None, None]
     )
     own_gain = transfer(defocus[0], blurring[0], squared)
-    received_real = lax.all_to_all(spec_real, "pix", split_axis=3, concat_axis=3, tiled=True)
+    s_next = lax.axis_size("pix")
+    taken_in, everything = (s_next, lax.axis_index("pix"))
+    wide_out = _note_leaves(spec_real, 3, taken_in)
+    local_part = wide_out
+    no = 1
+    while no < taken_in:
+        z_new, b_now = ((everything + no) % taken_in, (everything - no) % taken_in)
+        outcome_arr = lax.dynamic_index_in_dim(wide_out, z_new, 0)
+        current_value = lax.ppermute(
+            outcome_arr, "pix", [(pp, (pp + no) % taken_in) for pp in range(taken_in)]
+        )
+        local_part = lax.dynamic_update_slice_in_dim(local_part, current_value, b_now, axis=0)
+        no += 1
+    received_real = process_ways(local_part, 3)
     received_imaginary = lax.all_to_all(spec_imag, "pix", split_axis=3, concat_axis=3, tiled=True)
     middle_real, middle_imaginary = complex_product(
         "uhqb,bn->uhqn", received_real, received_imaginary, pixel_lookup_table

time: 497 us -> 520 us (1.046)
  local copies, waits for them, and re-layouts: 33.6 us -> 61.3 us
  starting transfers between devices: 20.2 us -> 31.5 us
  matrix products: 147 us -> 137 us
  waiting for transfers between devices: 260 us -> 253 us
    all_to_all x1, waiting for transfers between devices: 38.4 us -> 0.01 us  [body(): lax.all_to_all(spec_imag, 'pix', split_axis=3, concat_axis=3, tiled=True)]
    ppermute x0 -> x7, waiting for transfers between devices: none -> 37.2 us  [body(): lax.ppermute(outcome_arr, 'pix', [(pp, (pp + no) % taken_in) for pp in ra...]
    dynamic_update_slice x0 -> x7, local copies, waits for them, and re-layouts: none -> 27.4 us  [body(): lax.dynamic_update_slice_in_dim(local_part, current_value, b_now, axis=0)]
    all_to_all x1 -> x0, waiting for transfers between devices: 25.6 us -> none  [body(): lax.all_to_all(spec_real, 'pix', split_axis=3, concat_axis=3, tiled=True)]
    psum x1, waiting for transfers between devices: 119 us -> 139 us  [body(): totals = lax.psum((summands[0], summands[1], summands[2]), 'dist')]
    ppermute x0 -> x7, starting transfers between devices: none -> 14.7 us  [body(): lax.ppermute(outcome_arr, 'pix', [(pp, (pp + no) % taken_in) for pp in ra...]
  transfers between devices with their start and end apart: 5 -> 11, of which waited for: 5 -> 5; matrix products, arithmetic and copies ran while one was open for 10% -> 13% of each run, Pallas kernels for 0% -> 0%
where the time goes in v1:
time: 520 us; the launch traced here: 513 us
  waiting for transfers between devices  253 us (49%)
  matrix products  137 us (26%)
  local copies, waits for them, and re-layouts  61.3 us (12%)
  starting transfers between devices  31.5 us (6%)
  between operations  15.9 us (3%)
  other arithmetic  14.3 us (3%)
    psum x1, waiting for transfers between devices, body(): totals = lax.psum((summands[0], summands[1], summands[2]), 'dist')  139 us
    all_to_all x1, waiting for transfers between devices, body(): lax.all_to_all(backward_real, 'pix', split_axis=3, concat_axis=3, tiled=T...  40.4 us
    dot_general x7, matrix products, complex_product(): jnp.einsum(pattern, real_part, sine_part, precision=lax.Precision.HIGHEST)  38.6 us
    ppermute x7, waiting for transfers between devices, body(): lax.ppermute(outcome_arr, 'pix', [(pp, (pp + no) % taken_in) for pp in ra...  37.2 us
    all_to_all x1, waiting for transfers between devices, body(): lax.all_to_all(backward_imaginary, 'pix', split_axis=3, concat_axis=3, ti...  36.2 us
    dot_general x7, matrix products, complex_product(): jnp.einsum(pattern, real_part, cosine, precision=lax.Precision.HIGHEST)  35.1 us
    dynamic_update_slice x7, local copies, waits for them, and re-layouts, body(): lax.dynamic_update_slice_in_dim(local_part, current_value, b_now, axis=0)  27.4 us
    dot_general x7, matrix products, complex_product(): jnp.einsum(pattern, imag_part, sine_part, precision=lax.Precision.HIGHEST)  26 us
  transfers between devices with their start and end apart: 11, of which 5 were waited for; matrix products, arithmetic and copies ran while one was open for 13% of the time, Pallas kernels for 0%

profile of v1, /device:TPU:0, one launch (start us, length us, event | category | flops | bytes accessed | tf_op | source)
XLA Modules:
  0.0 512.6 jit_solution(8094186534501393537)
XLA Ops:
  6.6 3.9 fusion.321
  14.3 4.2 fusion.101
  18.5 4.2 fusion.89
  27.9 4.7 convolution_subtract_fusion
  32.6 3.6 multiply_subtract_fusion.2
  39.4 3.6 add_bitcast_fusion.1
  45.0 7.4 %all-to-all-start = ((f32[1,256,256,8]{2,1,0,3:T(8,128)}), f32[1,256,256,8]{2,1,0,3:T(8,128)}, u32[]{:S(2)}, u32[]{:S(2)}) async-start(f32[1,256,256,8]{2,1,0,3:T(8,128)} %copy.92), calls=%async_computation | async-start | bytes 4194304 | tf_op jit(solution)/shard_map/all_to_all | solution.py:110
  72.3 26.1 %collective-permute-done = f32[1,1,256,256,1]{3,0,2,4,1:T(1,128)S(1)} collective-permute-done((f32[1,1,256,256,1]{3,0,2,4,1:T(1,128)}, f32[1,1,256,256,1]{3,0,2,4,1:T(1,128)S(1)}, u32[]{:S(2)}, u32[]{:S(2)}) %collective-permute-start) | collective-permute-done | bytes 262176 | tf_op jit(solution)/shard_map/ppermute | solution.py:104
  98.4 5.2 %collective-permute-start.6 = (f32[1,1,256,256,1]{3,0,2,4,1:T(1,128)}, f32[1,1,256,256,1]{3,0,2,4,1:T(1,128)}, u32[]{:S(2)}, u32[]{:S(2)}) collective-permute-start(f32[1,1,256,256,1]{3,0,2,4,1:T(1,128)} %get-tuple-element.18), channel_id=1, source_target_pairs={{0,7},{1,0},{2,1},{3,2},{4,3},{5,4},{6,5},{7,6},{8,15},{9,8},{10,9... | collective-permute-start | bytes 786440 | tf_op jit(solution)/shard_map/ppermute | solution.py:104
  103.6 9.3 %fusion.79 = f32[1,256,256,8]{1,2,3,0:T(8,128)} fusion(f32[]{:T(128)} %bitcast.218, f32[256]{0:T(256)S(1)} %fusion.220, f32[256,8]{0,1:T(8,128)S(1)} %multiply_multiply_fusion, f32[]{:T(128)} %bitcast.2), kind=kLoop, calls=%fused_computation.90 | loop fusion | flops 3670016 | bytes 2106376 | tf_op jit(solution)/shard_map/mul | solution.py:118
  116.3 3.4 dynamic_update_slice.22
  119.7 11.1 %collective-permute-done.2 = f32[1,1,256,256,1]{3,0,2,4,1:T(1,128)S(1)} collective-permute-done((f32[1,1,256,256,1]{3,0,2,4,1:T(1,128)}, f32[1,1,256,256,1]{3,0,2,4,1:T(1,128)S(1)}, u32[]{:S(2)}, u32[]{:S(2)}) %collective-permute-start.2) | collective-permute-done | bytes 262176 | tf_op jit(solution)/shard_map/ppermute | solution.py:104
  134.2 3.4 dynamic_update_slice.24
  141.1 5.1 dynamic_update_slice.26
  146.2 5.3 %dynamic_update_slice.27 = f32[8,1,256,256,1]{3,0,2,4,1:T(8,128)S(1)} dynamic-update-slice(f32[8,1,256,256,1]{3,0,2,4,1:T(8,128)S(1)} %dynamic_update_slice.26, f32[1,1,256,256,1]{3,0,2,4,1:T(1,128)} %collective-permute-done.6, s32[]{:T(128)S(6)} %select_n.265, s32[]{:T(128)} %constant.165.clone.1, s32[]{:T(128)} %constant.165.clone.1, s32[]{:T(128)} %constant.165.clone.1, s32[]{:T(128)} %constant.165.clone.1) | dynamic-update-slice | bytes 524292 | tf_op jit(solution)/shard_map/dynamic_update_slice | solution.py:107
  151.4 4.7 fusion.32
  158.1 4.7 fusion.30
  165.4 3.5 fusion.40
  172.1 13.1 %bitcast_multiply_fusion.1 = f32[1,256,256,8]{1,2,3,0:T(8,128)} fusion(f32[256,256,8]{1,0,2:T(8,128)S(1)} %fusion.40, f32[256,256,8]{1,2,0:T(8,128)S(1)} %get-tuple-element.12, f32[]{:T(128)} %bitcast.217, f32[256]{0:T(256)S(1)} %fusion.220, f32[256,8]{0,1:T(8,128)S(1)} %multiply_multiply_fusion, f32[]{:T(128)} %bitcast.2), kind=kOutput, calls=%fused_computation.10 | convolution fusion | flops 1615724544 | bytes 6300680 | tf_op jit(solution)/shard_map/pcrk,rj->pcjk/dot_general | solution.py:37
  185.2 12.9 %bitcast_multiply_fusion = f32[1,256,256,8]{1,2,3,0:T(8,128)} fusion(f32[256,256,8]{1,0,2:T(8,128)S(1)} %fusion.38, f32[256,256,8]{1,2,0:T(8,128)S(1)} %get-tuple-element.12, f32[]{:T(128)} %bitcast.219, f32[256]{0:T(256)S(1)} %fusion.220, f32[256,8]{0,1:T(8,128)S(1)} %multiply_multiply_fusion, f32[]{:T(128)} %bitcast.2), kind=kOutput, calls=%fused_computation.9 | convolution fusion | flops 1615790080 | bytes 6300680 | tf_op jit(solution)/shard_map/pcrk,rj->pcjk/dot_general | solution.py:40
  198.2 139.2 %all-reduce.3.cloned.1.call-done = (f32[1,256,256,8]{1,2,3,0:T(8,128)}, f32[1,256,256,8]{1,2,3,0:T(8,128)}, f32[1,256,256,8]{1,2,3,0:T(8,128)}) async-done(((f32[1,256,256,8]{1,2,3,0:T(8,128)}, f32[1,256,256,8]{1,2,3,0:T(8,128)}, f32[1,256,256,8]{1,2,3,0:T(8,128)}), (f32[1,256,256,8]{1,2,3,0:T(8,128)}, f32[1,256,256,8]{1,2,3,0:T(8,128)}, f32[1,256,256,8]{1,2,3,0:T(8,128)})) %all-reduce.3.cloned.1.call-update) | async-done | bytes 6291472 | tf_op jit(solution)/shard_map/psum | solution.py:119
  337.4 5.4 %fusion.18 = f32[256,256,8]{1,0,2:T(8,128)S(1)} fusion(f32[1,256,256,8]{1,2,3,0:T(8,128)} %get-tuple-element.5, f32[1,256,256,8]{1,2,3,0:T(8,128)} %get-tuple-element.6), kind=kOutput, calls=%fused_computation.27 | convolution fusion | flops 1613103104 | bytes 6291456 | tf_op jit(solution)/shard_map/pcjk,rj->pcrk/dot_general | solution.py:42
  349.4 5.7 %fusion.17 = (f32[256,256,8]{0,1,2:T(8,128)}, f32[256,256,8]{0,1,2:T(8,128)}) fusion(f32[256,256,8]{1,0,2:T(8,128)S(1)} %fusion.73, f32[256,8]{0,1:T(8,128)S(1)} %fusion.159, f32[256,8]{0,1:T(8,128)S(1)} %get-tuple-element.25, f32[256,256,8]{1,0,2:T(8,128)S(1)} %fusion.18, f32[1,256,256,8]{1,2,3,0:T(8,128)S(1)} %copy-done.9, ...), kind=kOutput, calls=%fused_computation.24 | convolution fusion | flops 1616773120 | bytes 12599296 | tf_op jit(solution)/shard_map/pcjk,rj->pcrk/dot_general | solution.py:40
  363.2 3.6 multiply_bitcast_fusion.1
  368.8 5.5 %all-to-all-start.1 = ((f32[1,256,256,8]{2,1,0,3:T(8,128)}), f32[1,256,256,8]{2,1,0,3:T(8,128)}, u32[]{:S(2)}, u32[]{:S(2)}) async-start(f32[1,256,256,8]{2,1,0,3:T(8,128)} %copy.111), calls=%async_computation.1 | async-start | bytes 4194304 | tf_op jit(solution)/shard_map/all_to_all | solution.py:137
  374.3 3.5 fusion.141
  381.9 40.4 %all-to-all-done.1 = f32[1,256,256,8]{2,1,0,3:T(8,128)} async-done(((f32[1,256,256,8]{2,1,0,3:T(8,128)}), f32[1,256,256,8]{2,1,0,3:T(8,128)}, u32[]{:S(2)}, u32[]{:S(2)}) %all-to-all-start.1) | async-done | bytes 2097184 | tf_op jit(solution)/shard_map/all_to_all | solution.py:137
  422.3 3.8 all-to-all-start.2
  426.1 6.1 %fusion.10 = f32[256,256,8]{1,2,0:T(8,128)} fusion(f32[1,256,256,8]{2,1,0,3:T(8,128)} %all-to-all-done.1), kind=kOutput, calls=%fused_computation.15 | convolution fusion | flops 50332544 | bytes 4194304 | tf_op jit(solution)/shard_map/pcrq,nq->pcrn/dot_general | solution.py:40
  432.2 5.9 %fusion.12 = f32[256,256,8]{1,2,0:T(8,128)} fusion(f32[1,256,256,8]{2,1,0,3:T(8,128)} %all-to-all-done.1), kind=kOutput, calls=%fused_computation.17 | convolution fusion | flops 50332544 | bytes 4194304 | tf_op jit(solution)/shard_map/pcrq,nq->pcrn/dot_general | solution.py:37
  438.1 36.2 %all-to-all-done.2 = f32[1,256,256,8]{2,1,0,3:T(8,128)S(1)} async-done(((f32[1,256,256,8]{2,1,0,3:T(8,128)}), f32[1,256,256,8]{2,1,0,3:T(8,128)S(1)}, u32[]{:S(2)}, u32[]{:S(2)}) %all-to-all-start.2) | async-done | bytes 2097184 | tf_op jit(solution)/shard_map/all_to_all | solution.py:138
  500.0 5.3 %copy.123 = f32[2,256,2048]{2,1,0:T(8,128)} copy(f32[2,256,2048]{1,2,0:T(8,128)} %maximum_multiply_fusion) | data formatting | bytes 8388608 | tf_op jit(solution)/shard_map/div | solution.py:154
  (74 shorter events, 96.5 us)
Async XLA Ops:
  27.9 4.7 copy-start.5
  36.2 3.2 copy-start.2
  36.2 3.2 copy-start
  45.0 7.6 %copy-start.3 = (f32[256,256,8]{1,0,2:T(8,128)S(1)}, f32[256,256,8]{1,0,2:T(8,128)}, u32[]{:S(2)}) copy-start(f32[256,256,8]{1,0,2:T(8,128)} %copy-done.2) | copy-start | bytes 6291460
  45.0 106.4 %all-to-all-start = ((f32[1,256,256,8]{2,1,0,3:T(8,128)}), f32[1,256,256,8]{2,1,0,3:T(8,128)}, u32[]{:S(2)}, u32[]{:S(2)}) async-start(f32[1,256,256,8]{2,1,0,3:T(8,128)} %copy.92), calls=%async_computation | async-start | bytes 4194304 | tf_op jit(solution)/shard_map/all_to_all | solution.py:110
  52.5 284.9 %all-reduce.3.cloned.1.call-start = ((), (), s32[]{:S(2)}) async-start(), calls=%async_computation.3 | async-start | bytes 12582912 | tf_op jit(solution)/shard_map/psum | solution.py:119
  52.6 3.1 copy-start.1
  61.3 37.1 %collective-permute-start = (f32[1,1,256,256,1]{3,0,2,4,1:T(1,128)}, f32[1,1,256,256,1]{3,0,2,4,1:T(1,128)S(1)}, u32[]{:S(2)}, u32[]{:S(2)}) collective-permute-start(f32[1,1,256,256,1]{3,0,2,4,1:T(1,128)} %get-tuple-element.24), channel_id=1, source_target_pairs={{0,1},{1,2},{2,3},{3,4},{4,5},{5,6},{6,7},{7,0},{8,9},{9,10},{10,1... | collective-permute-start | bytes 786440 | tf_op jit(solution)/shard_map/ppermute | solution.py:104
  63.1 35.3 %collective-permute-start.1 = (f32[1,1,256,256,1]{3,0,2,4,1:T(1,128)}, f32[1,1,256,256,1]{3,0,2,4,1:T(1,128)S(1)}, u32[]{:S(2)}, u32[]{:S(2)}) collective-permute-start(f32[1,1,256,256,1]{3,0,2,4,1:T(1,128)} %get-tuple-element.23), channel_id=1, source_target_pairs={{0,2},{1,3},{2,4},{3,5},{4,6},{5,7},{6,0},{7,1},{8,10},{9,11},{10,... | collective-permute-start | bytes 786440 | tf_op jit(solution)/shard_map/ppermute | solution.py:104
  64.6 66.2 %collective-permute-start.2 = (f32[1,1,256,256,1]{3,0,2,4,1:T(1,128)}, f32[1,1,256,256,1]{3,0,2,4,1:T(1,128)S(1)}, u32[]{:S(2)}, u32[]{:S(2)}) collective-permute-start(f32[1,1,256,256,1]{3,0,2,4,1:T(1,128)} %get-tuple-element.22), channel_id=1, source_target_pairs={{0,3},{1,4},{2,5},{3,6},{4,7},{5,0},{6,1},{7,2},{8,11},{9,12},{10,... | collective-permute-start | bytes 786440 | tf_op jit(solution)/shard_map/ppermute | solution.py:104
  67.0 67.2 %collective-permute-start.3 = (f32[1,1,256,256,1]{3,0,2,4,1:T(1,128)}, f32[1,1,256,256,1]{3,0,2,4,1:T(1,128)S(1)}, u32[]{:S(2)}, u32[]{:S(2)}) collective-permute-start(f32[1,1,256,256,1]{3,0,2,4,1:T(1,128)} %get-tuple-element.21), channel_id=1, source_target_pairs={{0,4},{1,5},{2,6},{3,7},{4,0},{5,1},{6,2},{7,3},{8,12},{9,13},{10,... | collective-permute-start | bytes 786440 | tf_op jit(solution)/shard_map/ppermute | solution.py:104
  68.4 69.2 %collective-permute-start.4 = (f32[1,1,256,256,1]{3,0,2,4,1:T(1,128)}, f32[1,1,256,256,1]{3,0,2,4,1:T(1,128)S(1)}, u32[]{:S(2)}, u32[]{:S(2)}) collective-permute-start(f32[1,1,256,256,1]{3,0,2,4,1:T(1,128)} %get-tuple-element.20), channel_id=1, source_target_pairs={{0,5},{1,6},{2,7},{3,0},{4,1},{5,2},{6,3},{7,4},{8,13},{9,14},{10,... | collective-permute-start | bytes 786440 | tf_op jit(solution)/shard_map/ppermute | solution.py:104
  98.4 42.7 %collective-permute-start.5 = (f32[1,1,256,256,1]{3,0,2,4,1:T(1,128)}, f32[1,1,256,256,1]{3,0,2,4,1:T(1,128)}, u32[]{:S(2)}, u32[]{:S(2)}) collective-permute-start(f32[1,1,256,256,1]{3,0,2,4,1:T(1,128)} %get-tuple-element.19), channel_id=1, source_target_pairs={{0,6},{1,7},{2,0},{3,1},{4,2},{5,3},{6,4},{7,5},{8,14},{9,15},{10,... | collective-permute-start | bytes 786440 | tf_op jit(solution)/shard_map/ppermute | solution.py:104
  98.4 47.8 %collective-permute-start.6 = (f32[1,1,256,256,1]{3,0,2,4,1:T(1,128)}, f32[1,1,256,256,1]{3,0,2,4,1:T(1,128)}, u32[]{:S(2)}, u32[]{:S(2)}) collective-permute-start(f32[1,1,256,256,1]{3,0,2,4,1:T(1,128)} %get-tuple-element.18), channel_id=1, source_target_pairs={{0,7},{1,0},{2,1},{3,2},{4,3},{5,4},{6,5},{7,6},{8,15},{9,8},{10,9... | collective-permute-start | bytes 786440 | tf_op jit(solution)/shard_map/ppermute | solution.py:104
  337.4 5.5 %copy-start.8 = (f32[1,256,256,8]{1,2,3,0:T(8,128)S(1)}, f32[1,256,256,8]{1,2,3,0:T(8,128)}, u32[]{:S(2)}) copy-start(f32[1,256,256,8]{1,2,3,0:T(8,128)} %get-tuple-element.6) | copy-start | bytes 6291460
  337.4 5.5 %copy-start.10 = (f32[1,256,256,8]{1,2,3,0:T(8,128)S(1)}, f32[1,256,256,8]{1,2,3,0:T(8,128)}, u32[]{:S(2)}) copy-start(f32[1,256,256,8]{1,2,3,0:T(8,128)} %get-tuple-element.5) | copy-start | bytes 6291460
  342.9 3.1 copy-start.9
  357.3 3.2 copy-start.4
  368.8 53.5 %all-to-all-start.1 = ((f32[1,256,256,8]{2,1,0,3:T(8,128)}), f32[1,256,256,8]{2,1,0,3:T(8,128)}, u32[]{:S(2)}, u32[]{:S(2)}) async-start(f32[1,256,256,8]{2,1,0,3:T(8,128)} %copy.111), calls=%async_computation.1 | async-start | bytes 4194304 | tf_op jit(solution)/shard_map/all_to_all | solution.py:137
  422.3 52.1 %all-to-all-start.2 = ((f32[1,256,256,8]{2,1,0,3:T(8,128)}), f32[1,256,256,8]{2,1,0,3:T(8,128)S(1)}, u32[]{:S(2)}, u32[]{:S(2)}) async-start(f32[1,256,256,8]{2,1,0,3:T(8,128)} %copy.115), calls=%async_computation.2 | async-start | bytes 4194304 | tf_op jit(solution)/shard_map/all_to_all | solution.py:138
  477.4 3.3 copy-start.6
  477.4 3.3 copy-start.7
Sparse Core Ops, SparseCore 0:
  198.2 139.0 all-reduce.2
